TPU v7x, 128 devices: a whole 4x4x4 slice. The times are simulated.
128 devices in a mesh: res: 32 (over z, x, core), grp: 4 (over y).
Axes of the slice: x: 4, y: 4, z: 4, core: 2. Of those that a mesh axis runs over, the one named last changes fastest.
Arguments:
- right_side: float32 [3, 64, 64, 512], P(None, 'res', 'grp'), may hold values from -30 to 30
- accumulation: float32 [3, 3, 64, 64, 512], P(None, None, 'res', 'grp'), may hold values from -1 to 2, as said below
- transmissibility: float32 [6, 3, 3, 64, 64, 512], P(None, None, None, 'res', 'grp'), may hold values from -1 to 2, as said below
- completion: int32 [1024, 256], P(('res', 'grp')), may hold values from 0 to 16383, as said below
- live_count: int32 [1024], P(('res', 'grp')), may hold values from 64 to 256
- owner: int32 [1024, 1], P(('res', 'grp')), may hold values from 0 to 3; in each aligned block of 8 rows (0 to 7, 8 to 15, ...) at most 4 rows name the same one
- cell_to_well: float32 [1024, 3, 256], P(('res', 'grp')), may hold values from -3 to 3
- well_to_cell: float32 [1024, 3, 256], P(('res', 'grp')), may hold values from -3 to 3
- inverse: float32 [128, 4, 4, 256, 256], P(('res', 'grp')), may hold values from -1 to 2
Outputs:
- solution: float32 [3, 64, 64, 512], P(None, 'res', 'grp')
- residual: float32 [3, 64, 64, 512], P(None, 'res', 'grp')
Inputs may be any that keep to these rules, and one draw needn't show every extreme that they name: `completion`: cells may repeat. Among the 8 wells of one device at most 4 name the same owner. `accumulation`: diagonal entries positive. `transmissibility`: diagonal entries positive.
All inputs are finite; a program needn't handle non-finite values.
Results may differ from a plain program's by a relative error of at most 0.0003.
Values sent between devices are 32-bit elements; how exact they have to be, the bound alone decides.
A program may use at most 128 MiB of HBM per device.

v0:
```python
import jax
import jax.numpy as jnp
from jax import lax
from jax.sharding import Mesh
from jax.sharding import PartitionSpec as P

ITERS = 3
RES_GRP = ("res_0", "res_1", "res_2", "grp")
RES = ("res_0", "res_1", "res_2")


def extended(shard, sides, width):
    edges = {}
    for axis, dim in sides:
        devices, length = (lax.axis_size(axis), shard.shape[dim])
        up = [(i, (i + 1) % devices) for i in range(devices - 1)]
        last = lax.slice_in_dim(shard, length - width, length, axis=dim)
        leading = lax.slice_in_dim(shard, 0, width, axis=dim)
        edges[dim] = (
            lax.ppermute(last, axis, up),
            lax.ppermute(leading, axis, [(b, a) for a, b in up]),
        )
    done = []
    for _, dim in sides:
        low, high = edges[dim]
        around = [(width, width) if d in done else (0, 0) for d in range(shard.ndim)]
        shard = jnp.concatenate([jnp.pad(low, around), shard, jnp.pad(high, around)], axis=dim)
        done.append(dim)
    return shard


def over_axes(shard, axes):
    for axis in axes:
        shard = lax.psum(shard, axis)
    return shard


def neighbours(vector):
    padded = extended(vector, ((RES, 1), ("grp", 2)), 1)
    zpadded = jnp.pad(vector, ((0, 0), (0, 0), (0, 0), (1, 1)))
    return [
        padded[:, 2:, 1:-1, :],
        padded[:, :-2, 1:-1, :],
        padded[:, 1:-1, 2:, :],
        padded[:, 1:-1, :-2, :],
        zpadded[..., 2:],
        zpadded[..., :-2],
    ]


def stencil(vector, diag_total, transmissibility):
    beside_list = neighbours(vector)
    result = jnp.sum(diag_total * vector[None], axis=1)
    for face in range(6):
        result = result - jnp.sum(transmissibility[face] * beside_list[face][None], axis=1)
    return result


def body(
    right_side,
    accumulation,
    transmissibility,
    completion,
    live_count,
    owner,
    cell_to_well,
    well_to_cell,
    inverse,
):
    highest = lax.Precision.HIGHEST
    components, cells_x, cells_y, cells_z = right_side.shape
    blocks, segb = completion.shape
    capacity = inverse.shape[2]
    groups = lax.axis_size("grp")
    flat_index = completion.reshape(-1)
    open_mask = (jnp.arange(segb, dtype=jnp.int32)[None, :] < live_count[:, None]).astype(
        jnp.float32
    )
    owner_eq = (owner == jnp.arange(groups, dtype=jnp.int32)[None, :]).astype(jnp.int32)
    prior = jnp.cumsum(owner_eq, axis=0) - owner_eq
    slot_number = jnp.sum(prior * owner_eq, axis=1)
    target = owner[:, 0] * capacity + slot_number
    packing = (target[:, None] == jnp.arange(groups * capacity, dtype=jnp.int32)[None, :]).astype(
        jnp.float32
    )
    diag_total = accumulation
    for face in range(6):
        diag_total = diag_total + transmissibility[face]
    moved = lax.all_to_all(inverse[0], "grp", split_axis=0, concat_axis=0, tiled=True)
    block_inverse = jnp.einsum(
        "bq,qst->bst", packing, moved.reshape(groups * capacity, segb, segb), precision=highest
    )

    def solve_wells(coupled):
        return jnp.einsum("bst,bt->bs", block_inverse, coupled, precision=highest)

    def operator(vector):
        result = stencil(vector, diag_total, transmissibility)
        flat = vector.reshape(components, -1)
        picked = jnp.moveaxis(flat[:, flat_index].reshape(components, blocks, segb), 0, 1)
        coupled = jnp.sum(cell_to_well * picked, axis=1) * open_mask
        well_value = solve_wells(coupled)
        correction = well_to_cell * (well_value * open_mask)[:, None, :]
        correction = jnp.moveaxis(correction, 0, 1).reshape(components, -1)
        out_flat = result.reshape(components, -1).at[:, flat_index].add(-correction)
        return out_flat.reshape(vector.shape)

    solution = jnp.zeros_like(right_side)
    residual = right_side
    search = right_side
    rho = over_axes(jnp.sum(residual * residual), RES_GRP)
    for index in range(ITERS):
        image = operator(search)
        alpha = rho / over_axes(jnp.sum(right_side * image), RES_GRP)
        middle = residual - alpha * image
        second = operator(middle)
        inner, square, along_middle, along_second = (
            over_axes(jnp.sum(second * middle), RES_GRP),
            over_axes(jnp.sum(second * second), RES_GRP),
            over_axes(jnp.sum(right_side * middle), RES_GRP),
            over_axes(jnp.sum(right_side * second), RES_GRP),
        )
        omega = inner / square
        solution = solution + alpha * search + omega * middle
        residual = middle - omega * second
        rho_next = along_middle - omega * along_second
        if index + 1 < ITERS:
            search = residual + rho_next / rho * (alpha / omega) * (search - omega * image)
            rho = rho_next
    return (solution, residual)


def solution(mesh):
    finer = Mesh(
        mesh.devices.reshape(4, 4, 2, mesh.shape["grp"]), ("res_0", "res_1", "res_2", "grp")
    )
    in_specs = (
        P(None, RES, "grp", None),
        P(None, None, RES, "grp", None),
        P(None, None, None, RES, "grp", None),
        P(RES_GRP, None),
        P(RES_GRP),
        P(RES_GRP, None),
        P(RES_GRP, None, None),
        P(RES_GRP, None, None),
        P(RES_GRP, None, None, None, None),
    )
    out_specs = (P(None, RES, "grp", None), P(None, RES, "grp", None))
    return jax.shard_map(body, mesh=finer, in_specs=in_specs, out_specs=out_specs, check_vma=False)
```

profile of v0, /device:TPU:10, one launch (start us, length us, event | category | flops | bytes accessed | tf_op | source)
XLA Modules:
  0.0 719.2 jit_solution(10837892056741657385)
XLA Ops:
  27.1 11.0 %gather_fusion = f32[2048,3]{1,0:T(8,128)} fusion(f32[3,16384]{0,1:T(8,128)} %bitcast.284, s32[2048]{0:T(1024)S(1)} %broadcast_clamp_fusion), kind=kCustom, calls=%fused_computation | custom fusion | bytes 57344 | tf_op jit(solution)/shard_map/gather | solution.py:100
  60.8 6.0 fusion
  74.2 17.4 %scatter_fusion = f32[3,16384]{0,1:T(8,128)} fusion(f32[3,16384]{0,1:T(8,128)} %bitcast.273, s32[2048]{0:T(1024)S(1)} %bitcast.299, f32[2048,3]{1,0:T(8,128)} %bitcast.291), kind=kCustom, calls=%fused_computation.6 | custom fusion | flops 6144 | bytes 81920 | tf_op jit(solution)/shard_map/scatter-add | solution.py:105
  91.6 5.9 copy.92
  99.1 12.4 %all-reduce.29 = (f32[]{:T(128)}, f32[]{:T(128)}) all-reduce(f32[]{:T(128)} %get-tuple-element.45, f32[]{:T(128)} %get-tuple-element.44), channel_id=1, replica_groups=mesh['res_0'=4,'res_1'=4,'res_2'=2,'grp'=4] {'res_0'}, use_global_device_ids=true, to_apply=%region_1.2 | all-reduce | flops 2 | bytes 16 | tf_op jit(solution)/shard_map/psum | solution.py:34
  111.6 11.0 %all-reduce.25 = (f32[]{:T(128)}, f32[]{:T(128)}) all-reduce(f32[]{:T(128)} %get-tuple-element.80, f32[]{:T(128)} %get-tuple-element.81), channel_id=1, replica_groups=mesh['res_0'=4,'res_1'=4,'res_2'=2,'grp'=4] {'res_1'}, use_global_device_ids=true, to_apply=%region_2.3 | all-reduce | flops 2 | bytes 16 | tf_op jit(solution)/shard_map/psum | solution.py:34
  125.8 8.7 %all-reduce.21 = (f32[]{:T(128)}, f32[]{:T(128)}) all-reduce(f32[]{:T(128)} %get-tuple-element.92, f32[]{:T(128)} %get-tuple-element.93), channel_id=1, replica_groups=mesh['res_0'=4,'res_1'=4,'res_2'=2,'grp'=4] {'grp'}, use_global_device_ids=true, to_apply=%region_4.5 | all-reduce | flops 2 | bytes 16 | tf_op jit(solution)/shard_map/psum | solution.py:34
  156.2 10.9 %gather_fusion.1 = f32[2048,3]{1,0:T(8,128)} fusion(f32[3,16384]{0,1:T(8,128)} %bitcast.280, s32[2048]{0:T(1024)S(1)} %broadcast_clamp_fusion), kind=kCustom, calls=%fused_computation.1 | custom fusion | bytes 57344 | tf_op jit(solution)/shard_map/gather | solution.py:100
  190.4 17.3 %scatter_fusion.1 = f32[3,16384]{0,1:T(8,128)} fusion(f32[3,16384]{0,1:T(8,128)} %bitcast.269, s32[2048]{0:T(1024)S(1)} %bitcast.300, f32[2048,3]{1,0:T(8,128)} %bitcast.288), kind=kCustom, calls=%fused_computation.7 | custom fusion | flops 6144 | bytes 81920 | tf_op jit(solution)/shard_map/scatter-add | solution.py:105
  220.6 8.4 %all-reduce.28 = (f32[]{:T(128)}, f32[]{:T(128)}, f32[]{:T(128)}, f32[]{:T(128)}) all-reduce(f32[]{:T(128)} %get-tuple-element.43, f32[]{:T(128)} %get-tuple-element.42, f32[]{:T(128)} %multiply_reduce_fusion.2, f32[]{:T(128)} %get-tuple-element.41), channel_id=1, replica_groups=mesh['res_0'=4,'res_1'=4,'res_2'=2,'grp'=4] {'res_0'}, use_global_device_ids=true, to_apply=%region_41.42 | all-reduce | flops 4 | bytes 32 | tf_op jit(solution)/shard_map/psum | solution.py:34
  229.1 11.5 %all-reduce.24 = (f32[]{:T(128)}, f32[]{:T(128)}, f32[]{:T(128)}, f32[]{:T(128)}) all-reduce(f32[]{:T(128)} %get-tuple-element.76, f32[]{:T(128)} %get-tuple-element.77, f32[]{:T(128)} %get-tuple-element.78, f32[]{:T(128)} %get-tuple-element.79), channel_id=1, replica_groups=mesh['res_0'=4,'res_1'=4,'res_2'=2,'grp'=4] {'res_1'}, use_global_device_ids=true, to_apply=%region_42.43 | all-reduce | flops 4 | bytes 32 | tf_op jit(solution)/shard_map/psum | solution.py:34
  243.8 8.1 %all-reduce.20 = (f32[]{:T(128)}, f32[]{:T(128)}, f32[]{:T(128)}, f32[]{:T(128)}) all-reduce(f32[]{:T(128)} %get-tuple-element.88, f32[]{:T(128)} %get-tuple-element.89, f32[]{:T(128)} %get-tuple-element.90, f32[]{:T(128)} %get-tuple-element.91), channel_id=1, replica_groups=mesh['res_0'=4,'res_1'=4,'res_2'=2,'grp'=4] {'grp'}, use_global_device_ids=true, to_apply=%region_44.45 | all-reduce | flops 4 | bytes 32 | tf_op jit(solution)/shard_map/psum | solution.py:34
  278.2 10.9 %gather_fusion.2 = f32[2048,3]{1,0:T(8,128)} fusion(f32[3,16384]{0,1:T(8,128)} %bitcast.281, s32[2048]{0:T(1024)S(1)} %broadcast_clamp_fusion), kind=kCustom, calls=%fused_computation.2 | custom fusion | bytes 57344 | tf_op jit(solution)/shard_map/gather | solution.py:100
  312.6 17.3 %scatter_fusion.2 = f32[3,16384]{0,1:T(8,128)} fusion(f32[3,16384]{0,1:T(8,128)} %bitcast.275, s32[2048]{0:T(1024)S(1)} %bitcast.301, f32[2048,3]{1,0:T(8,128)} %bitcast.289), kind=kCustom, calls=%fused_computation.8 | custom fusion | flops 6144 | bytes 81920 | tf_op jit(solution)/shard_map/scatter-add | solution.py:105
  337.4 8.9 %psum.416 = f32[]{:T(128)} all-reduce(f32[]{:T(128)} %multiply_reduce_fusion.14), channel_id=1, replica_groups=mesh['res_0'=4,'res_1'=4,'res_2'=2,'grp'=4] {'res_0'}, use_global_device_ids=true, to_apply=%region_60.61 | all-reduce | flops 1 | bytes 8 | tf_op jit(solution)/shard_map/psum | solution.py:34
  346.3 11.5 %psum.417 = f32[]{:T(128)} all-reduce(f32[]{:T(128)} %psum.416), channel_id=1, replica_groups=mesh['res_0'=4,'res_1'=4,'res_2'=2,'grp'=4] {'res_1'}, use_global_device_ids=true, to_apply=%region_61.62 | all-reduce | flops 1 | bytes 8 | tf_op jit(solution)/shard_map/psum | solution.py:34
  361.0 8.1 %psum.419 = f32[]{:T(128)} all-reduce(f32[]{:T(128)} %psum.418), channel_id=1, replica_groups=mesh['res_0'=4,'res_1'=4,'res_2'=2,'grp'=4] {'grp'}, use_global_device_ids=true, to_apply=%region_63.64 | all-reduce | flops 1 | bytes 8 | tf_op jit(solution)/shard_map/psum | solution.py:34
  390.2 10.9 %gather_fusion.3 = f32[2048,3]{1,0:T(8,128)} fusion(f32[3,16384]{0,1:T(8,128)} %bitcast.282, s32[2048]{0:T(1024)S(1)} %broadcast_clamp_fusion), kind=kCustom, calls=%fused_computation.3 | custom fusion | bytes 57344 | tf_op jit(solution)/shard_map/gather | solution.py:100
  424.4 17.3 %scatter_fusion.3 = f32[3,16384]{0,1:T(8,128)} fusion(f32[3,16384]{0,1:T(8,128)} %bitcast.271, s32[2048]{0:T(1024)S(1)} %bitcast.302, f32[2048,3]{1,0:T(8,128)} %bitcast.290), kind=kCustom, calls=%fused_computation.9 | custom fusion | flops 6144 | bytes 81920 | tf_op jit(solution)/shard_map/scatter-add | solution.py:105
  454.7 8.4 %all-reduce.27 = (f32[]{:T(128)}, f32[]{:T(128)}, f32[]{:T(128)}, f32[]{:T(128)}) all-reduce(f32[]{:T(128)} %get-tuple-element.40, f32[]{:T(128)} %get-tuple-element.39, f32[]{:T(128)} %multiply_reduce_fusion.1, f32[]{:T(128)} %get-tuple-element.38), channel_id=1, replica_groups=mesh['res_0'=4,'res_1'=4,'res_2'=2,'grp'=4] {'res_0'}, use_global_device_ids=true, to_apply=%region_84.85 | all-reduce | flops 4 | bytes 32 | tf_op jit(solution)/shard_map/psum | solution.py:34
  463.1 11.2 %all-reduce.23 = (f32[]{:T(128)}, f32[]{:T(128)}, f32[]{:T(128)}, f32[]{:T(128)}) all-reduce(f32[]{:T(128)} %get-tuple-element.72, f32[]{:T(128)} %get-tuple-element.73, f32[]{:T(128)} %get-tuple-element.74, f32[]{:T(128)} %get-tuple-element.75), channel_id=1, replica_groups=mesh['res_0'=4,'res_1'=4,'res_2'=2,'grp'=4] {'res_1'}, use_global_device_ids=true, to_apply=%region_85.86 | all-reduce | flops 4 | bytes 32 | tf_op jit(solution)/shard_map/psum | solution.py:34
  477.5 8.2 %all-reduce.19 = (f32[]{:T(128)}, f32[]{:T(128)}, f32[]{:T(128)}, f32[]{:T(128)}) all-reduce(f32[]{:T(128)} %get-tuple-element.84, f32[]{:T(128)} %get-tuple-element.85, f32[]{:T(128)} %get-tuple-element.86, f32[]{:T(128)} %get-tuple-element.87), channel_id=1, replica_groups=mesh['res_0'=4,'res_1'=4,'res_2'=2,'grp'=4] {'grp'}, use_global_device_ids=true, to_apply=%region_87.88 | all-reduce | flops 4 | bytes 32 | tf_op jit(solution)/shard_map/psum | solution.py:34
  510.9 10.9 %gather_fusion.4 = f32[2048,3]{1,0:T(8,128)} fusion(f32[3,16384]{0,1:T(8,128)} %bitcast.283, s32[2048]{0:T(1024)S(1)} %broadcast_clamp_fusion), kind=kCustom, calls=%fused_computation.4 | custom fusion | bytes 57344 | tf_op jit(solution)/shard_map/gather | solution.py:100
  545.1 17.3 %scatter_fusion.4 = f32[3,16384]{0,1:T(8,128)} fusion(f32[3,16384]{0,1:T(8,128)} %bitcast.277, s32[2048]{0:T(1024)S(1)} %bitcast.303, f32[2048,3]{1,0:T(8,128)} %bitcast.286), kind=kCustom, calls=%fused_computation.10 | custom fusion | flops 6144 | bytes 81920 | tf_op jit(solution)/shard_map/scatter-add | solution.py:105
  569.9 8.4 %psum.436 = f32[]{:T(128)} all-reduce(f32[]{:T(128)} %multiply_reduce_fusion.10), channel_id=1, replica_groups=mesh['res_0'=4,'res_1'=4,'res_2'=2,'grp'=4] {'res_0'}, use_global_device_ids=true, to_apply=%region_103.104 | all-reduce | flops 1 | bytes 8 | tf_op jit(solution)/shard_map/psum | solution.py:34
  578.4 11.9 %psum.437 = f32[]{:T(128)} all-reduce(f32[]{:T(128)} %psum.436), channel_id=1, replica_groups=mesh['res_0'=4,'res_1'=4,'res_2'=2,'grp'=4] {'res_1'}, use_global_device_ids=true, to_apply=%region_104.105 | all-reduce | flops 1 | bytes 8 | tf_op jit(solution)/shard_map/psum | solution.py:34
  593.4 8.1 %psum.439 = f32[]{:T(128)} all-reduce(f32[]{:T(128)} %psum.438), channel_id=1, replica_groups=mesh['res_0'=4,'res_1'=4,'res_2'=2,'grp'=4] {'grp'}, use_global_device_ids=true, to_apply=%region_106.107 | all-reduce | flops 1 | bytes 8 | tf_op jit(solution)/shard_map/psum | solution.py:34
  622.3 10.9 %gather_fusion.5 = f32[2048,3]{1,0:T(8,128)} fusion(f32[3,16384]{0,1:T(8,128)} %bitcast.279, s32[2048]{0:T(1024)S(1)} %broadcast_clamp_fusion), kind=kCustom, calls=%fused_computation.5 | custom fusion | bytes 57344 | tf_op jit(solution)/shard_map/gather | solution.py:100
  654.9 17.3 %scatter_fusion.5 = f32[3,16384]{0,1:T(8,128)} fusion(f32[3,16384]{0,1:T(8,128)} %bitcast.267, s32[2048]{0:T(1024)S(1)} %bitcast.304, f32[2048,3]{1,0:T(8,128)} %bitcast.287), kind=kCustom, calls=%fused_computation.11 | custom fusion | flops 6144 | bytes 81920 | tf_op jit(solution)/shard_map/scatter-add | solution.py:105
  683.3 8.4 %all-reduce.26 = (f32[]{:T(128)}, f32[]{:T(128)}) all-reduce(f32[]{:T(128)} %multiply_reduce_fusion.9, f32[]{:T(128)} %multiply_reduce_fusion), channel_id=1, replica_groups=mesh['res_0'=4,'res_1'=4,'res_2'=2,'grp'=4] {'res_0'}, use_global_device_ids=true, to_apply=%region_117.118 | all-reduce | flops 2 | bytes 16 | tf_op jit(solution)/shard_map/psum | solution.py:34
  691.7 11.0 %all-reduce.22 = (f32[]{:T(128)}, f32[]{:T(128)}) all-reduce(f32[]{:T(128)} %get-tuple-element.70, f32[]{:T(128)} %get-tuple-element.71), channel_id=1, replica_groups=mesh['res_0'=4,'res_1'=4,'res_2'=2,'grp'=4] {'res_1'}, use_global_device_ids=true, to_apply=%region_118.119 | all-reduce | flops 2 | bytes 16 | tf_op jit(solution)/shard_map/psum | solution.py:34
  705.7 11.0 %all-reduce.18 = (f32[]{:T(128)}, f32[]{:T(128)}) all-reduce(f32[]{:T(128)} %get-tuple-element.82, f32[]{:T(128)} %get-tuple-element.83), channel_id=1, replica_groups=mesh['res_0'=4,'res_1'=4,'res_2'=2,'grp'=4] {'grp'}, use_global_device_ids=true, to_apply=%region_120.121 | all-reduce | flops 2 | bytes 16 | tf_op jit(solution)/shard_map/psum | solution.py:34
  (210 shorter events, 346.7 us)
Async XLA Ops:
  0.6 45.1 %copy-start = (f32[6,3,3,2,16,512]{5,4,3,2,1,0:T(8,128)S(1)}, f32[6,3,3,2,16,512]{5,4,3,2,1,0:T(8,128)}, u32[]{:S(2)}) copy-start(f32[6,3,3,2,16,512]{5,4,3,2,1,0:T(8,128)} %param.11) | copy-start | bytes 10616836
  0.7 60.2 %all-to-all-start = ((f32[4,4,256,256]{3,2,1,0:T(8,128)}), f32[4,4,256,256]{3,2,1,0:T(8,128)}, u32[]{:S(2)}, u32[]{:S(2)}) async-start(f32[4,4,256,256]{3,2,1,0:T(8,128)} %bitcast.285), calls=%async_computation | async-start | bytes 8388608 | tf_op jit(solution)/shard_map/all_to_all | solution.py:89
  7.8 45.1 %collective-permute-start.3 = (f32[3,2,1,512]{3,2,1,0:T(1,128)}, f32[3,2,1,512]{3,2,1,0:T(1,128)}, u32[]{:S(2)}, u32[]{:S(2)}) collective-permute-start(f32[3,2,1,512]{3,2,1,0:T(1,128)} %get-tuple-element.171), channel_id=1, source_target_pairs={{0,1},{1,2},{2,3},{4,5},{5,6},{6,7},{8,9},{9,10},{10,11},{12,13},{... | collective-permute-start | bytes 36872 | tf_op jit(solution)/shard_map/ppermute | solution.py:20
  11.2 41.8 %collective-permute-start.2 = (f32[3,2,1,512]{3,2,1,0:T(1,128)}, f32[3,2,1,512]{3,2,1,0:T(1,128)}, u32[]{:S(2)}, u32[]{:S(2)}) collective-permute-start(f32[3,2,1,512]{3,2,1,0:T(1,128)} %get-tuple-element.172), channel_id=1, source_target_pairs={{1,0},{2,1},{3,2},{5,4},{6,5},{7,6},{9,8},{10,9},{11,10},{13,12},{... | collective-permute-start | bytes 36872 | tf_op jit(solution)/shard_map/ppermute | solution.py:21
  15.9 33.6 %collective-permute-start.1 = (f32[3,1,16,512]{3,2,1,0:T(8,128)}, f32[3,1,16,512]{3,2,1,0:T(8,128)}, u32[]{:S(2)}, u32[]{:S(2)}) collective-permute-start(f32[3,1,16,512]{3,2,1,0:T(8,128)} %get-tuple-element.173), channel_id=1, source_target_pairs={{0,4},{4,8},{8,12},{12,16},{16,20},{20,24},{24,28},{28,32},{32,36}... | collective-permute-start | bytes 294920 | tf_op jit(solution)/shard_map/ppermute | solution.py:20
  17.8 32.6 %collective-permute-start = (f32[3,1,16,512]{3,2,1,0:T(8,128)}, f32[3,1,16,512]{3,2,1,0:T(8,128)}, u32[]{:S(2)}, u32[]{:S(2)}) collective-permute-start(f32[3,1,16,512]{3,2,1,0:T(8,128)} %get-tuple-element.174), channel_id=1, source_target_pairs={{4,0},{8,4},{12,8},{16,12},{20,16},{24,20},{28,24},{32,28},{36,32}... | collective-permute-start | bytes 294920 | tf_op jit(solution)/shard_map/ppermute | solution.py:21
  143.9 36.9 %collective-permute-start.7 = (f32[3,2,1,512]{3,2,1,0:T(1,128)}, f32[3,2,1,512]{3,2,1,0:T(1,128)}, u32[]{:S(2)}, u32[]{:S(2)}) collective-permute-start(f32[3,2,1,512]{3,2,1,0:T(1,128)} %get-tuple-element.162), channel_id=1, source_target_pairs={{0,1},{1,2},{2,3},{4,5},{5,6},{6,7},{8,9},{9,10},{10,11},{12,13},{... | collective-permute-start | bytes 36872 | tf_op jit(solution)/shard_map/ppermute | solution.py:20
  147.5 33.2 %collective-permute-start.6 = (f32[3,2,1,512]{3,2,1,0:T(1,128)}, f32[3,2,1,512]{3,2,1,0:T(1,128)}, u32[]{:S(2)}, u32[]{:S(2)}) collective-permute-start(f32[3,2,1,512]{3,2,1,0:T(1,128)} %get-tuple-element.163), channel_id=1, source_target_pairs={{1,0},{2,1},{3,2},{5,4},{6,5},{7,6},{9,8},{10,9},{11,10},{13,12},{... | collective-permute-start | bytes 36872 | tf_op jit(solution)/shard_map/ppermute | solution.py:21
  150.6 30.1 %collective-permute-start.5 = (f32[3,1,16,512]{3,2,1,0:T(8,128)}, f32[3,1,16,512]{3,2,1,0:T(8,128)}, u32[]{:S(2)}, u32[]{:S(2)}) collective-permute-start(f32[3,1,16,512]{3,2,1,0:T(8,128)} %get-tuple-element.164), channel_id=1, source_target_pairs={{0,4},{4,8},{8,12},{12,16},{16,20},{20,24},{24,28},{28,32},{32,36}... | collective-permute-start | bytes 294920 | tf_op jit(solution)/shard_map/ppermute | solution.py:20
  152.6 28.2 %collective-permute-start.4 = (f32[3,1,16,512]{3,2,1,0:T(8,128)}, f32[3,1,16,512]{3,2,1,0:T(8,128)}, u32[]{:S(2)}, u32[]{:S(2)}) collective-permute-start(f32[3,1,16,512]{3,2,1,0:T(8,128)} %get-tuple-element.165), channel_id=1, source_target_pairs={{4,0},{8,4},{12,8},{16,12},{20,16},{24,20},{28,24},{32,28},{36,32}... | collective-permute-start | bytes 294920 | tf_op jit(solution)/shard_map/ppermute | solution.py:21
  265.9 36.8 %collective-permute-start.11 = (f32[3,2,1,512]{3,2,1,0:T(1,128)}, f32[3,2,1,512]{3,2,1,0:T(1,128)}, u32[]{:S(2)}, u32[]{:S(2)}) collective-permute-start(f32[3,2,1,512]{3,2,1,0:T(1,128)} %get-tuple-element.152), channel_id=1, source_target_pairs={{0,1},{1,2},{2,3},{4,5},{5,6},{6,7},{8,9},{9,10},{10,11},{12,13},{... | collective-permute-start | bytes 36872 | tf_op jit(solution)/shard_map/ppermute | solution.py:20
  269.0 33.7 %collective-permute-start.10 = (f32[3,2,1,512]{3,2,1,0:T(1,128)}, f32[3,2,1,512]{3,2,1,0:T(1,128)}, u32[]{:S(2)}, u32[]{:S(2)}) collective-permute-start(f32[3,2,1,512]{3,2,1,0:T(1,128)} %get-tuple-element.153), channel_id=1, source_target_pairs={{1,0},{2,1},{3,2},{5,4},{6,5},{7,6},{9,8},{10,9},{11,10},{13,12},{... | collective-permute-start | bytes 36872 | tf_op jit(solution)/shard_map/ppermute | solution.py:21
  272.4 30.4 %collective-permute-start.9 = (f32[3,1,16,512]{3,2,1,0:T(8,128)}, f32[3,1,16,512]{3,2,1,0:T(8,128)}, u32[]{:S(2)}, u32[]{:S(2)}) collective-permute-start(f32[3,1,16,512]{3,2,1,0:T(8,128)} %get-tuple-element.154), channel_id=1, source_target_pairs={{0,4},{4,8},{8,12},{12,16},{16,20},{20,24},{24,28},{28,32},{32,36}... | collective-permute-start | bytes 294920 | tf_op jit(solution)/shard_map/ppermute | solution.py:20
  274.3 28.4 %collective-permute-start.8 = (f32[3,1,16,512]{3,2,1,0:T(8,128)}, f32[3,1,16,512]{3,2,1,0:T(8,128)}, u32[]{:S(2)}, u32[]{:S(2)}) collective-permute-start(f32[3,1,16,512]{3,2,1,0:T(8,128)} %get-tuple-element.155), channel_id=1, source_target_pairs={{4,0},{8,4},{12,8},{16,12},{20,16},{24,20},{28,24},{32,28},{36,32}... | collective-permute-start | bytes 294920 | tf_op jit(solution)/shard_map/ppermute | solution.py:21
  377.9 36.8 %collective-permute-start.15 = (f32[3,2,1,512]{3,2,1,0:T(1,128)}, f32[3,2,1,512]{3,2,1,0:T(1,128)}, u32[]{:S(2)}, u32[]{:S(2)}) collective-permute-start(f32[3,2,1,512]{3,2,1,0:T(1,128)} %get-tuple-element.142), channel_id=1, source_target_pairs={{0,1},{1,2},{2,3},{4,5},{5,6},{6,7},{8,9},{9,10},{10,11},{12,13},{... | collective-permute-start | bytes 36872 | tf_op jit(solution)/shard_map/ppermute | solution.py:20
  380.9 33.8 %collective-permute-start.14 = (f32[3,2,1,512]{3,2,1,0:T(1,128)}, f32[3,2,1,512]{3,2,1,0:T(1,128)}, u32[]{:S(2)}, u32[]{:S(2)}) collective-permute-start(f32[3,2,1,512]{3,2,1,0:T(1,128)} %get-tuple-element.143), channel_id=1, source_target_pairs={{1,0},{2,1},{3,2},{5,4},{6,5},{7,6},{9,8},{10,9},{11,10},{13,12},{... | collective-permute-start | bytes 36872 | tf_op jit(solution)/shard_map/ppermute | solution.py:21
  384.4 30.4 %collective-permute-start.13 = (f32[3,1,16,512]{3,2,1,0:T(8,128)}, f32[3,1,16,512]{3,2,1,0:T(8,128)}, u32[]{:S(2)}, u32[]{:S(2)}) collective-permute-start(f32[3,1,16,512]{3,2,1,0:T(8,128)} %get-tuple-element.144), channel_id=1, source_target_pairs={{0,4},{4,8},{8,12},{12,16},{16,20},{20,24},{24,28},{28,32},{32,36}... | collective-permute-start | bytes 294920 | tf_op jit(solution)/shard_map/ppermute | solution.py:20
  386.3 28.5 %collective-permute-start.12 = (f32[3,1,16,512]{3,2,1,0:T(8,128)}, f32[3,1,16,512]{3,2,1,0:T(8,128)}, u32[]{:S(2)}, u32[]{:S(2)}) collective-permute-start(f32[3,1,16,512]{3,2,1,0:T(8,128)} %get-tuple-element.145), channel_id=1, source_target_pairs={{4,0},{8,4},{12,8},{16,12},{20,16},{24,20},{28,24},{32,28},{36,32}... | collective-permute-start | bytes 294920 | tf_op jit(solution)/shard_map/ppermute | solution.py:21
  498.5 37.0 %collective-permute-start.19 = (f32[3,2,1,512]{3,2,1,0:T(1,128)}, f32[3,2,1,512]{3,2,1,0:T(1,128)}, u32[]{:S(2)}, u32[]{:S(2)}) collective-permute-start(f32[3,2,1,512]{3,2,1,0:T(1,128)} %get-tuple-element.132), channel_id=1, source_target_pairs={{0,1},{1,2},{2,3},{4,5},{5,6},{6,7},{8,9},{9,10},{10,11},{12,13},{... | collective-permute-start | bytes 36872 | tf_op jit(solution)/shard_map/ppermute | solution.py:20
  501.4 34.0 %collective-permute-start.18 = (f32[3,2,1,512]{3,2,1,0:T(1,128)}, f32[3,2,1,512]{3,2,1,0:T(1,128)}, u32[]{:S(2)}, u32[]{:S(2)}) collective-permute-start(f32[3,2,1,512]{3,2,1,0:T(1,128)} %get-tuple-element.133), channel_id=1, source_target_pairs={{1,0},{2,1},{3,2},{5,4},{6,5},{7,6},{9,8},{10,9},{11,10},{13,12},{... | collective-permute-start | bytes 36872 | tf_op jit(solution)/shard_map/ppermute | solution.py:21
  504.9 30.6 %collective-permute-start.17 = (f32[3,1,16,512]{3,2,1,0:T(8,128)}, f32[3,1,16,512]{3,2,1,0:T(8,128)}, u32[]{:S(2)}, u32[]{:S(2)}) collective-permute-start(f32[3,1,16,512]{3,2,1,0:T(8,128)} %get-tuple-element.134), channel_id=1, source_target_pairs={{0,4},{4,8},{8,12},{12,16},{16,20},{20,24},{24,28},{28,32},{32,36}... | collective-permute-start | bytes 294920 | tf_op jit(solution)/shard_map/ppermute | solution.py:20
  506.8 28.7 %collective-permute-start.16 = (f32[3,1,16,512]{3,2,1,0:T(8,128)}, f32[3,1,16,512]{3,2,1,0:T(8,128)}, u32[]{:S(2)}, u32[]{:S(2)}) collective-permute-start(f32[3,1,16,512]{3,2,1,0:T(8,128)} %get-tuple-element.135), channel_id=1, source_target_pairs={{4,0},{8,4},{12,8},{16,12},{20,16},{24,20},{28,24},{32,28},{36,32}... | collective-permute-start | bytes 294920 | tf_op jit(solution)/shard_map/ppermute | solution.py:21
  610.4 36.5 %collective-permute-start.22 = (f32[3,2,1,512]{3,2,1,0:T(1,128)}, f32[3,2,1,512]{3,2,1,0:T(1,128)}, u32[]{:S(2)}, u32[]{:S(2)}) collective-permute-start(f32[3,2,1,512]{3,2,1,0:T(1,128)} %get-tuple-element.122), channel_id=1, source_target_pairs={{1,0},{2,1},{3,2},{5,4},{6,5},{7,6},{9,8},{10,9},{11,10},{13,12},{... | collective-permute-start | bytes 36872 | tf_op jit(solution)/shard_map/ppermute | solution.py:21
  614.6 32.3 %collective-permute-start.23 = (f32[3,2,1,512]{3,2,1,0:T(1,128)}, f32[3,2,1,512]{3,2,1,0:T(1,128)}, u32[]{:S(2)}, u32[]{:S(2)}) collective-permute-start(f32[3,2,1,512]{3,2,1,0:T(1,128)} %get-tuple-element.123), channel_id=1, source_target_pairs={{0,1},{1,2},{2,3},{4,5},{5,6},{6,7},{8,9},{9,10},{10,11},{12,13},{... | collective-permute-start | bytes 36872 | tf_op jit(solution)/shard_map/ppermute | solution.py:20
  616.5 30.4 %collective-permute-start.21 = (f32[3,1,16,512]{3,2,1,0:T(8,128)}, f32[3,1,16,512]{3,2,1,0:T(8,128)}, u32[]{:S(2)}, u32[]{:S(2)}) collective-permute-start(f32[3,1,16,512]{3,2,1,0:T(8,128)} %get-tuple-element.124), channel_id=1, source_target_pairs={{0,4},{4,8},{8,12},{12,16},{16,20},{20,24},{24,28},{28,32},{32,36}... | collective-permute-start | bytes 294920 | tf_op jit(solution)/shard_map/ppermute | solution.py:20
  618.5 28.5 %collective-permute-start.20 = (f32[3,1,16,512]{3,2,1,0:T(8,128)}, f32[3,1,16,512]{3,2,1,0:T(8,128)}, u32[]{:S(2)}, u32[]{:S(2)}) collective-permute-start(f32[3,1,16,512]{3,2,1,0:T(8,128)} %get-tuple-element.125), channel_id=1, source_target_pairs={{4,0},{8,4},{12,8},{16,12},{20,16},{24,20},{28,24},{32,28},{36,32}... | collective-permute-start | bytes 294920 | tf_op jit(solution)/shard_map/ppermute | solution.py:21
  672.1 45.9 %copy-start.2 = (f32[3,2,16,512]{3,2,1,0:T(8,128)S(1)}, f32[3,2,16,512]{3,2,1,0:T(8,128)}, u32[]{:S(2)}) copy-start(f32[3,2,16,512]{3,2,1,0:T(8,128)} %param.9) | copy-start | bytes 589828
  672.1 45.9 %copy-start.4 = (f32[3,2,16,512]{3,2,1,0:T(8,128)S(1)}, f32[3,2,16,512]{3,2,1,0:T(8,128)}, u32[]{:S(2)}) copy-start(f32[3,2,16,512]{3,2,1,0:T(8,128)} %copy-done.3) | copy-start | bytes 589828
  672.2 45.9 %copy-start.6 = (f32[3,2,16,512]{3,2,1,0:T(8,128)S(1)}, f32[3,2,16,512]{3,2,1,0:T(8,128)}, u32[]{:S(2)}) copy-start(f32[3,2,16,512]{3,2,1,0:T(8,128)} %copy-done.5) | copy-start | bytes 589828
  672.2 45.9 %copy-start.8 = (f32[3,2,16,512]{3,2,1,0:T(8,128)S(1)}, f32[3,2,16,512]{3,2,1,0:T(8,128)}, u32[]{:S(2)}) copy-start(f32[3,2,16,512]{3,2,1,0:T(8,128)} %copy-done.7) | copy-start | bytes 589828
  672.2 45.9 %copy-start.12 = (f32[3,2,16,512]{3,2,1,0:T(8,128)S(1)}, f32[3,2,16,512]{3,2,1,0:T(8,128)}, u32[]{:S(2)}) copy-start(f32[3,2,16,512]{3,2,1,0:T(8,128)} %copy.106) | copy-start | bytes 589828
  672.2 45.9 %copy-start.13 = (f32[3,2,16,512]{3,2,1,0:T(8,128)S(1)}, f32[3,2,16,512]{3,2,1,0:T(8,128)}, u32[]{:S(2)}) copy-start(f32[3,2,16,512]{3,2,1,0:T(8,128)} %copy.112) | copy-start | bytes 589828
  (10 other events, 62.9 us)
where the time goes:
time: 734 us; the launch traced here: 719 us
  local copies, waits for them, and re-layouts  205 us (28%)
  other arithmetic  196 us (27%)
  blocking collectives  194 us (26%)
  starting transfers between devices  78.5 us (11%)
  matrix products  28.8 us (4%)
  between operations  15.8 us (2%)
    psum x24, blocking collectives, over_axes(): shard = lax.psum(shard, axis)  194 us
    scatter-add x6, other arithmetic, operator(): out_flat = result.reshape(components, -1).at[:, flat_index].add(-correction)  104 us
    gather x6, local copies, waits for them, and re-layouts, operator(): flat[:, flat_index].reshape(components, blocks, segb)  65.7 us
    ppermute x12, starting transfers between devices, extended(): lax.ppermute(leading, axis, [(b, a) for a, b in up])  43.5 us
    reshape x6, local copies, waits for them, and re-layouts, operator(): return out_flat.reshape(vector.shape)  34.5 us
    sub x6, local copies, waits for them, and re-layouts, stencil(): result - jnp.sum(transmissibility[face] * beside_list[face][None], axis=1)  32.8 us
    ppermute x12, starting transfers between devices, extended(): lax.ppermute(last, axis, up)  29.4 us
    dot_general x6, matrix products, solve_wells(): return jnp.einsum('bst,bt->bs', block_inverse, coupled, precision=highest)  22.8 us
  transfers between devices with their start and end apart: 25, of which 0 were waited for; matrix products, arithmetic and copies ran while one was open for 23% of the time, Pallas kernels for 0%

commit v1 on v0

--- a/solution.py
+++ b/solution.py
@@ -31,7 +31,7 @@
 
 def over_axes(shard, axes):
     for axis in axes:
-        shard = lax.psum(shard, axis)
+        shard = jnp.sum(lax.all_gather(shard, axis), axis=0)
     return shard
 
 

time: 734 us -> 971 us (1.32)
  local copies, waits for them, and re-layouts: 205 us -> 377 us
  other arithmetic: 196 us -> 268 us
  starting transfers between devices: 78.5 us -> 68.2 us
    psum x24 -> x0, blocking collectives: 194 us -> none  [over_axes(): shard = lax.psum(shard, axis)]
    unnamed x0 -> x24, blocking collectives: none -> 194 us
    unnamed x37 -> x145, local copies, waits for them, and re-layouts: 8 us -> 170 us
    reduce_sum x0 -> x56, other arithmetic: none -> 67.5 us  [over_axes(): shard = jnp.sum(lax.all_gather(shard, axis), axis=0)]
    ppermute x12, starting transfers between devices: 43.5 us -> 28.6 us  [extended(): lax.ppermute(leading, axis, [(b, a) for a, b in up])]
  transfers between devices with their start and end apart: 25 -> 25, of which waited for: 0 -> 0; matrix products, arithmetic and copies ran while one was open for 23% -> 7% of each run, Pallas kernels for 0% -> 0%
where the time goes in v1:
time: 971 us; the launch traced here: 953 us
  local copies, waits for them, and re-layouts  377 us (39%)
  other arithmetic  268 us (28%)
  blocking collectives  194 us (20%)
  starting transfers between devices  68.2 us (7%)
  matrix products  28.8 us (3%)
  between operations  16.6 us (2%)
    unnamed x24, blocking collectives  194 us
    unnamed x145, local copies, waits for them, and re-layouts  170 us
    scatter-add x6, other arithmetic, operator(): out_flat = result.reshape(components, -1).at[:, flat_index].add(-correction)  104 us
    reduce_sum x56, other arithmetic, over_axes(): shard = jnp.sum(lax.all_gather(shard, axis), axis=0)  67.5 us
    gather x6, local copies, waits for them, and re-layouts, operator(): flat[:, flat_index].reshape(components, blocks, segb)  65.6 us
    reshape x6, local copies, waits for them, and re-layouts, operator(): return out_flat.reshape(vector.shape)  34.5 us
    ppermute x12, starting transfers between devices, extended(): lax.ppermute(last, axis, up)  34 us
    sub x6, local copies, waits for them, and re-layouts, stencil(): result - jnp.sum(transmissibility[face] * beside_list[face][None], axis=1)  32.8 us
  transfers between devices with their start and end apart: 25, of which 0 were waited for; matrix products, arithmetic and copies ran while one was open for 7% of the time, Pallas kernels for 0%

profile of v1, /device:TPU:10, one launch (start us, length us, event | category | flops | bytes accessed | tf_op | source)
XLA Modules:
  0.0 952.8 jit_solution(675561980886700099)
XLA Ops:
  26.6 11.0 %gather_fusion = f32[2048,3]{1,0:T(8,128)} fusion(f32[3,16384]{0,1:T(8,128)} %bitcast.344, s32[2048]{0:T(1024)S(1)} %broadcast_clamp_fusion), kind=kCustom, calls=%fused_computation | custom fusion | bytes 57344 | tf_op jit(solution)/shard_map/gather | solution.py:100
  62.3 6.0 fusion
  75.7 17.5 %scatter_fusion = f32[3,16384]{0,1:T(8,128)} fusion(f32[3,16384]{0,1:T(8,128)} %bitcast.333, s32[2048]{0:T(1024)S(1)} %bitcast.359, f32[2048,3]{1,0:T(8,128)} %bitcast.351), kind=kCustom, calls=%fused_computation.6 | custom fusion | flops 6144 | bytes 81920 | tf_op jit(solution)/shard_map/scatter-add | solution.py:105
  93.1 5.9 copy.92
  108.3 12.5 %all-reduce.85 = (f32[4]{0:T(128)}, f32[4]{0:T(128)}) all-reduce(f32[4]{0:T(128)} %dynamic-update-slice, f32[4]{0:T(128)} %dynamic-update-slice.4), channel_id=1, replica_groups=mesh['res_0'=4,'res_1'=4,'res_2'=2,'grp'=4] {'res_0'}, use_global_device_ids=true, to_apply=%add.18 | all-reduce | flops 8 | bytes 64
  130.8 11.1 %all-reduce.81 = (f32[4]{0:T(128)}, f32[4]{0:T(128)}) all-reduce(f32[4]{0:T(128)} %dynamic-update-slice.1, f32[4]{0:T(128)} %dynamic-update-slice.5), channel_id=1, replica_groups=mesh['res_0'=4,'res_1'=4,'res_2'=2,'grp'=4] {'res_1'}, use_global_device_ids=true, to_apply=%add.19 | all-reduce | flops 8 | bytes 64
  164.1 9.8 %all-reduce.77 = (f32[4]{0:T(128)}, f32[4]{0:T(128)}) all-reduce(f32[4]{0:T(128)} %dynamic-update-slice.3, f32[4]{0:T(128)} %dynamic-update-slice.7), channel_id=1, replica_groups=mesh['res_0'=4,'res_1'=4,'res_2'=2,'grp'=4] {'grp'}, use_global_device_ids=true, to_apply=%add.21 | all-reduce | flops 8 | bytes 64
  188.5 10.9 %gather_fusion.1 = f32[2048,3]{1,0:T(8,128)} fusion(f32[3,16384]{0,1:T(8,128)} %bitcast.340, s32[2048]{0:T(1024)S(1)} %broadcast_clamp_fusion), kind=kCustom, calls=%fused_computation.1 | custom fusion | bytes 57344 | tf_op jit(solution)/shard_map/gather | solution.py:100
  232.9 17.3 %scatter_fusion.1 = f32[3,16384]{0,1:T(8,128)} fusion(f32[3,16384]{0,1:T(8,128)} %bitcast.329, s32[2048]{0:T(1024)S(1)} %bitcast.360, f32[2048,3]{1,0:T(8,128)} %bitcast.348), kind=kCustom, calls=%fused_computation.7 | custom fusion | flops 6144 | bytes 81920 | tf_op jit(solution)/shard_map/scatter-add | solution.py:105
  275.4 8.4 all-reduce.84
  300.6 9.7 %all-reduce.80 = (f32[4]{0:T(128)}, f32[4]{0:T(128)}, f32[4]{0:T(128)}, f32[4]{0:T(128)}) all-reduce(f32[4]{0:T(128)} %dynamic-update-slice.17, f32[4]{0:T(128)} %dynamic-update-slice.9, f32[4]{0:T(128)} %dynamic-update-slice.13, f32[4]{0:T(128)} %dynamic-update-slice.21), channel_id=1, replica_groups=mesh['res_0'=4,'res_1'=4,'res_2'=2,'grp'=4] {'res_1'}, use_global_device_ids=true, to_apply=%add.35 | all-reduce | flops 16 | bytes 128
  347.7 10.0 %all-reduce.76 = (f32[4]{0:T(128)}, f32[4]{0:T(128)}, f32[4]{0:T(128)}, f32[4]{0:T(128)}) all-reduce(f32[4]{0:T(128)} %dynamic-update-slice.19, f32[4]{0:T(128)} %dynamic-update-slice.11, f32[4]{0:T(128)} %dynamic-update-slice.15, f32[4]{0:T(128)} %dynamic-update-slice.23), channel_id=1, replica_groups=mesh['res_0'=4,'res_1'=4,'res_2'=2,'grp'=4] {'grp'}, use_global_device_ids=true, to_apply=%add.37 | all-reduce | flops 16 | bytes 128
  379.5 10.9 %gather_fusion.2 = f32[2048,3]{1,0:T(8,128)} fusion(f32[3,16384]{0,1:T(8,128)} %bitcast.341, s32[2048]{0:T(1024)S(1)} %broadcast_clamp_fusion), kind=kCustom, calls=%fused_computation.2 | custom fusion | bytes 57344 | tf_op jit(solution)/shard_map/gather | solution.py:100
  424.1 17.3 %scatter_fusion.2 = f32[3,16384]{0,1:T(8,128)} fusion(f32[3,16384]{0,1:T(8,128)} %bitcast.335, s32[2048]{0:T(1024)S(1)} %bitcast.361, f32[2048,3]{1,0:T(8,128)} %bitcast.349), kind=kCustom, calls=%fused_computation.8 | custom fusion | flops 6144 | bytes 81920 | tf_op jit(solution)/shard_map/scatter-add | solution.py:105
  452.2 10.4 %all-reduce.42 = f32[4]{0:T(128)} all-reduce(f32[4]{0:T(128)} %dynamic-update-slice.24), channel_id=1, replica_groups=mesh['res_0'=4,'res_1'=4,'res_2'=2,'grp'=4] {'res_0'}, use_global_device_ids=true, to_apply=%add.42 | all-reduce | flops 4 | bytes 32
  467.1 9.1 all-reduce.43
  488.5 9.8 %all-reduce.45 = f32[4]{0:T(128)} all-reduce(f32[4]{0:T(128)} %dynamic-update-slice.27), channel_id=1, replica_groups=mesh['res_0'=4,'res_1'=4,'res_2'=2,'grp'=4] {'grp'}, use_global_device_ids=true, to_apply=%add.45 | all-reduce | flops 4 | bytes 32
  511.1 10.9 %gather_fusion.3 = f32[2048,3]{1,0:T(8,128)} fusion(f32[3,16384]{0,1:T(8,128)} %bitcast.342, s32[2048]{0:T(1024)S(1)} %broadcast_clamp_fusion), kind=kCustom, calls=%fused_computation.3 | custom fusion | bytes 57344 | tf_op jit(solution)/shard_map/gather | solution.py:100
  555.7 17.3 %scatter_fusion.3 = f32[3,16384]{0,1:T(8,128)} fusion(f32[3,16384]{0,1:T(8,128)} %bitcast.331, s32[2048]{0:T(1024)S(1)} %bitcast.362, f32[2048,3]{1,0:T(8,128)} %bitcast.350), kind=kCustom, calls=%fused_computation.9 | custom fusion | flops 6144 | bytes 81920 | tf_op jit(solution)/shard_map/scatter-add | solution.py:105
  598.2 9.4 all-reduce.83
  624.5 10.0 %all-reduce.79 = (f32[4]{0:T(128)}, f32[4]{0:T(128)}, f32[4]{0:T(128)}, f32[4]{0:T(128)}) all-reduce(f32[4]{0:T(128)} %dynamic-update-slice.37, f32[4]{0:T(128)} %dynamic-update-slice.29, f32[4]{0:T(128)} %dynamic-update-slice.33, f32[4]{0:T(128)} %dynamic-update-slice.41), channel_id=1, replica_groups=mesh['res_0'=4,'res_1'=4,'res_2'=2,'grp'=4] {'res_1'}, use_global_device_ids=true, to_apply=%add.55 | all-reduce | flops 16 | bytes 128
  672.1 9.6 %all-reduce.75 = (f32[4]{0:T(128)}, f32[4]{0:T(128)}, f32[4]{0:T(128)}, f32[4]{0:T(128)}) all-reduce(f32[4]{0:T(128)} %dynamic-update-slice.39, f32[4]{0:T(128)} %dynamic-update-slice.31, f32[4]{0:T(128)} %dynamic-update-slice.35, f32[4]{0:T(128)} %dynamic-update-slice.43), channel_id=1, replica_groups=mesh['res_0'=4,'res_1'=4,'res_2'=2,'grp'=4] {'grp'}, use_global_device_ids=true, to_apply=%add.57 | all-reduce | flops 16 | bytes 128
  702.6 10.9 %gather_fusion.4 = f32[2048,3]{1,0:T(8,128)} fusion(f32[3,16384]{0,1:T(8,128)} %bitcast.343, s32[2048]{0:T(1024)S(1)} %broadcast_clamp_fusion), kind=kCustom, calls=%fused_computation.4 | custom fusion | bytes 57344 | tf_op jit(solution)/shard_map/gather | solution.py:100
  747.2 17.3 %scatter_fusion.4 = f32[3,16384]{0,1:T(8,128)} fusion(f32[3,16384]{0,1:T(8,128)} %bitcast.337, s32[2048]{0:T(1024)S(1)} %bitcast.363, f32[2048,3]{1,0:T(8,128)} %bitcast.346), kind=kCustom, calls=%fused_computation.10 | custom fusion | flops 6144 | bytes 81920 | tf_op jit(solution)/shard_map/scatter-add | solution.py:105
  775.3 10.4 %all-reduce.62 = f32[4]{0:T(128)} all-reduce(f32[4]{0:T(128)} %dynamic-update-slice.44), channel_id=1, replica_groups=mesh['res_0'=4,'res_1'=4,'res_2'=2,'grp'=4] {'res_0'}, use_global_device_ids=true, to_apply=%add.62 | all-reduce | flops 4 | bytes 32
  790.1 8.4 all-reduce.63
  810.8 9.8 %all-reduce.65 = f32[4]{0:T(128)} all-reduce(f32[4]{0:T(128)} %dynamic-update-slice.47), channel_id=1, replica_groups=mesh['res_0'=4,'res_1'=4,'res_2'=2,'grp'=4] {'grp'}, use_global_device_ids=true, to_apply=%add.65 | all-reduce | flops 4 | bytes 32
  833.3 10.9 %gather_fusion.5 = f32[2048,3]{1,0:T(8,128)} fusion(f32[3,16384]{0,1:T(8,128)} %bitcast.339, s32[2048]{0:T(1024)S(1)} %broadcast_clamp_fusion), kind=kCustom, calls=%fused_computation.5 | custom fusion | bytes 57344 | tf_op jit(solution)/shard_map/gather | solution.py:100
  876.1 17.5 %scatter_fusion.5 = f32[3,16384]{0,1:T(8,128)} fusion(f32[3,16384]{0,1:T(8,128)} %bitcast.327, s32[2048]{0:T(1024)S(1)} %bitcast.364, f32[2048,3]{1,0:T(8,128)} %bitcast.347), kind=kCustom, calls=%fused_computation.11 | custom fusion | flops 6144 | bytes 81920 | tf_op jit(solution)/shard_map/scatter-add | solution.py:105
  907.6 9.4 all-reduce.82
  920.7 9.2 all-reduce.78
  939.9 8.9 all-reduce.74
  (374 shorter events, 578.8 us)
Async XLA Ops:
  0.6 44.5 %copy-start = (f32[6,3,3,2,16,512]{5,4,3,2,1,0:T(8,128)S(1)}, f32[6,3,3,2,16,512]{5,4,3,2,1,0:T(8,128)}, u32[]{:S(2)}) copy-start(f32[6,3,3,2,16,512]{5,4,3,2,1,0:T(8,128)} %param.11) | copy-start | bytes 10616836
  0.7 61.7 %all-to-all-start = ((f32[4,4,256,256]{3,2,1,0:T(8,128)}), f32[4,4,256,256]{3,2,1,0:T(8,128)}, u32[]{:S(2)}, u32[]{:S(2)}) async-start(f32[4,4,256,256]{3,2,1,0:T(8,128)} %bitcast.345), calls=%async_computation | async-start | bytes 8388608 | tf_op jit(solution)/shard_map/all_to_all | solution.py:89
  7.9 43.1 %collective-permute-start.1 = (f32[3,1,16,512]{3,2,1,0:T(8,128)}, f32[3,1,16,512]{3,2,1,0:T(8,128)}, u32[]{:S(2)}, u32[]{:S(2)}) collective-permute-start(f32[3,1,16,512]{3,2,1,0:T(8,128)} %get-tuple-element.173), channel_id=1, source_target_pairs={{0,4},{4,8},{8,12},{12,16},{16,20},{20,24},{24,28},{28,32},{32,36}... | collective-permute-start | bytes 294920 | tf_op jit(solution)/shard_map/ppermute | solution.py:20
  9.8 42.0 %collective-permute-start = (f32[3,1,16,512]{3,2,1,0:T(8,128)}, f32[3,1,16,512]{3,2,1,0:T(8,128)}, u32[]{:S(2)}, u32[]{:S(2)}) collective-permute-start(f32[3,1,16,512]{3,2,1,0:T(8,128)} %get-tuple-element.174), channel_id=1, source_target_pairs={{4,0},{8,4},{12,8},{16,12},{20,16},{24,20},{28,24},{32,28},{36,32}... | collective-permute-start | bytes 294920 | tf_op jit(solution)/shard_map/ppermute | solution.py:21
  15.0 39.4 %collective-permute-start.2 = (f32[3,2,1,512]{3,2,1,0:T(1,128)}, f32[3,2,1,512]{3,2,1,0:T(1,128)}, u32[]{:S(2)}, u32[]{:S(2)}) collective-permute-start(f32[3,2,1,512]{3,2,1,0:T(1,128)} %get-tuple-element.172), channel_id=1, source_target_pairs={{1,0},{2,1},{3,2},{5,4},{6,5},{7,6},{9,8},{10,9},{11,10},{13,12},{... | collective-permute-start | bytes 36872 | tf_op jit(solution)/shard_map/ppermute | solution.py:21
  17.0 37.5 %collective-permute-start.3 = (f32[3,2,1,512]{3,2,1,0:T(1,128)}, f32[3,2,1,512]{3,2,1,0:T(1,128)}, u32[]{:S(2)}, u32[]{:S(2)}) collective-permute-start(f32[3,2,1,512]{3,2,1,0:T(1,128)} %get-tuple-element.171), channel_id=1, source_target_pairs={{0,1},{1,2},{2,3},{4,5},{5,6},{6,7},{8,9},{9,10},{10,11},{12,13},{... | collective-permute-start | bytes 36872 | tf_op jit(solution)/shard_map/ppermute | solution.py:20
  209.1 14.2 %collective-permute-start.4 = (f32[3,1,16,512]{3,2,1,0:T(8,128)}, f32[3,1,16,512]{3,2,1,0:T(8,128)}, u32[]{:S(2)}, u32[]{:S(2)}) collective-permute-start(f32[3,1,16,512]{3,2,1,0:T(8,128)} %get-tuple-element.165), channel_id=1, source_target_pairs={{4,0},{8,4},{12,8},{16,12},{20,16},{24,20},{28,24},{32,28},{36,32}... | collective-permute-start | bytes 294920 | tf_op jit(solution)/shard_map/ppermute | solution.py:21
  211.0 12.2 %collective-permute-start.5 = (f32[3,1,16,512]{3,2,1,0:T(8,128)}, f32[3,1,16,512]{3,2,1,0:T(8,128)}, u32[]{:S(2)}, u32[]{:S(2)}) collective-permute-start(f32[3,1,16,512]{3,2,1,0:T(8,128)} %get-tuple-element.164), channel_id=1, source_target_pairs={{0,4},{4,8},{8,12},{12,16},{16,20},{20,24},{24,28},{28,32},{32,36}... | collective-permute-start | bytes 294920 | tf_op jit(solution)/shard_map/ppermute | solution.py:20
  213.4 9.8 %collective-permute-start.6 = (f32[3,2,1,512]{3,2,1,0:T(1,128)}, f32[3,2,1,512]{3,2,1,0:T(1,128)}, u32[]{:S(2)}, u32[]{:S(2)}) collective-permute-start(f32[3,2,1,512]{3,2,1,0:T(1,128)} %get-tuple-element.163), channel_id=1, source_target_pairs={{1,0},{2,1},{3,2},{5,4},{6,5},{7,6},{9,8},{10,9},{11,10},{13,12},{... | collective-permute-start | bytes 36872 | tf_op jit(solution)/shard_map/ppermute | solution.py:21
  215.9 7.3 collective-permute-start.7
  400.1 14.2 %collective-permute-start.8 = (f32[3,1,16,512]{3,2,1,0:T(8,128)}, f32[3,1,16,512]{3,2,1,0:T(8,128)}, u32[]{:S(2)}, u32[]{:S(2)}) collective-permute-start(f32[3,1,16,512]{3,2,1,0:T(8,128)} %get-tuple-element.155), channel_id=1, source_target_pairs={{4,0},{8,4},{12,8},{16,12},{20,16},{24,20},{28,24},{32,28},{36,32}... | collective-permute-start | bytes 294920 | tf_op jit(solution)/shard_map/ppermute | solution.py:21
  402.0 12.2 %collective-permute-start.9 = (f32[3,1,16,512]{3,2,1,0:T(8,128)}, f32[3,1,16,512]{3,2,1,0:T(8,128)}, u32[]{:S(2)}, u32[]{:S(2)}) collective-permute-start(f32[3,1,16,512]{3,2,1,0:T(8,128)} %get-tuple-element.154), channel_id=1, source_target_pairs={{0,4},{4,8},{8,12},{12,16},{16,20},{20,24},{24,28},{28,32},{32,36}... | collective-permute-start | bytes 294920 | tf_op jit(solution)/shard_map/ppermute | solution.py:20
  404.4 9.8 %collective-permute-start.10 = (f32[3,2,1,512]{3,2,1,0:T(1,128)}, f32[3,2,1,512]{3,2,1,0:T(1,128)}, u32[]{:S(2)}, u32[]{:S(2)}) collective-permute-start(f32[3,2,1,512]{3,2,1,0:T(1,128)} %get-tuple-element.153), channel_id=1, source_target_pairs={{1,0},{2,1},{3,2},{5,4},{6,5},{7,6},{9,8},{10,9},{11,10},{13,12},{... | collective-permute-start | bytes 36872 | tf_op jit(solution)/shard_map/ppermute | solution.py:21
  407.2 7.0 collective-permute-start.11
  531.7 14.3 %collective-permute-start.12 = (f32[3,1,16,512]{3,2,1,0:T(8,128)}, f32[3,1,16,512]{3,2,1,0:T(8,128)}, u32[]{:S(2)}, u32[]{:S(2)}) collective-permute-start(f32[3,1,16,512]{3,2,1,0:T(8,128)} %get-tuple-element.145), channel_id=1, source_target_pairs={{4,0},{8,4},{12,8},{16,12},{20,16},{24,20},{28,24},{32,28},{36,32}... | collective-permute-start | bytes 294920 | tf_op jit(solution)/shard_map/ppermute | solution.py:21
  533.6 12.4 %collective-permute-start.13 = (f32[3,1,16,512]{3,2,1,0:T(8,128)}, f32[3,1,16,512]{3,2,1,0:T(8,128)}, u32[]{:S(2)}, u32[]{:S(2)}) collective-permute-start(f32[3,1,16,512]{3,2,1,0:T(8,128)} %get-tuple-element.144), channel_id=1, source_target_pairs={{0,4},{4,8},{8,12},{12,16},{16,20},{20,24},{24,28},{28,32},{32,36}... | collective-permute-start | bytes 294920 | tf_op jit(solution)/shard_map/ppermute | solution.py:20
  536.1 10.0 %collective-permute-start.14 = (f32[3,2,1,512]{3,2,1,0:T(1,128)}, f32[3,2,1,512]{3,2,1,0:T(1,128)}, u32[]{:S(2)}, u32[]{:S(2)}) collective-permute-start(f32[3,2,1,512]{3,2,1,0:T(1,128)} %get-tuple-element.143), channel_id=1, source_target_pairs={{1,0},{2,1},{3,2},{5,4},{6,5},{7,6},{9,8},{10,9},{11,10},{13,12},{... | collective-permute-start | bytes 36872 | tf_op jit(solution)/shard_map/ppermute | solution.py:21
  538.6 7.5 collective-permute-start.15
  723.2 14.4 %collective-permute-start.16 = (f32[3,1,16,512]{3,2,1,0:T(8,128)}, f32[3,1,16,512]{3,2,1,0:T(8,128)}, u32[]{:S(2)}, u32[]{:S(2)}) collective-permute-start(f32[3,1,16,512]{3,2,1,0:T(8,128)} %get-tuple-element.135), channel_id=1, source_target_pairs={{4,0},{8,4},{12,8},{16,12},{20,16},{24,20},{28,24},{32,28},{36,32}... | collective-permute-start | bytes 294920 | tf_op jit(solution)/shard_map/ppermute | solution.py:21
  725.1 12.5 %collective-permute-start.17 = (f32[3,1,16,512]{3,2,1,0:T(8,128)}, f32[3,1,16,512]{3,2,1,0:T(8,128)}, u32[]{:S(2)}, u32[]{:S(2)}) collective-permute-start(f32[3,1,16,512]{3,2,1,0:T(8,128)} %get-tuple-element.134), channel_id=1, source_target_pairs={{0,4},{4,8},{8,12},{12,16},{16,20},{20,24},{24,28},{28,32},{32,36}... | collective-permute-start | bytes 294920 | tf_op jit(solution)/shard_map/ppermute | solution.py:20
  727.6 10.0 %collective-permute-start.18 = (f32[3,2,1,512]{3,2,1,0:T(1,128)}, f32[3,2,1,512]{3,2,1,0:T(1,128)}, u32[]{:S(2)}, u32[]{:S(2)}) collective-permute-start(f32[3,2,1,512]{3,2,1,0:T(1,128)} %get-tuple-element.133), channel_id=1, source_target_pairs={{1,0},{2,1},{3,2},{5,4},{6,5},{7,6},{9,8},{10,9},{11,10},{13,12},{... | collective-permute-start | bytes 36872 | tf_op jit(solution)/shard_map/ppermute | solution.py:21
  730.3 7.2 collective-permute-start.19
  853.9 14.2 %collective-permute-start.20 = (f32[3,1,16,512]{3,2,1,0:T(8,128)}, f32[3,1,16,512]{3,2,1,0:T(8,128)}, u32[]{:S(2)}, u32[]{:S(2)}) collective-permute-start(f32[3,1,16,512]{3,2,1,0:T(8,128)} %get-tuple-element.125), channel_id=1, source_target_pairs={{4,0},{8,4},{12,8},{16,12},{20,16},{24,20},{28,24},{32,28},{36,32}... | collective-permute-start | bytes 294920 | tf_op jit(solution)/shard_map/ppermute | solution.py:21
  856.2 12.0 %collective-permute-start.21 = (f32[3,1,16,512]{3,2,1,0:T(8,128)}, f32[3,1,16,512]{3,2,1,0:T(8,128)}, u32[]{:S(2)}, u32[]{:S(2)}) collective-permute-start(f32[3,1,16,512]{3,2,1,0:T(8,128)} %get-tuple-element.124), channel_id=1, source_target_pairs={{0,4},{4,8},{8,12},{12,16},{16,20},{20,24},{24,28},{28,32},{32,36}... | collective-permute-start | bytes 294920 | tf_op jit(solution)/shard_map/ppermute | solution.py:20
  858.2 9.9 %collective-permute-start.22 = (f32[3,2,1,512]{3,2,1,0:T(1,128)}, f32[3,2,1,512]{3,2,1,0:T(1,128)}, u32[]{:S(2)}, u32[]{:S(2)}) collective-permute-start(f32[3,2,1,512]{3,2,1,0:T(1,128)} %get-tuple-element.122), channel_id=1, source_target_pairs={{1,0},{2,1},{3,2},{5,4},{6,5},{7,6},{9,8},{10,9},{11,10},{13,12},{... | collective-permute-start | bytes 36872 | tf_op jit(solution)/shard_map/ppermute | solution.py:21
  860.7 7.4 collective-permute-start.23
  893.6 57.8 %copy-start.2 = (f32[3,2,16,512]{3,2,1,0:T(8,128)S(1)}, f32[3,2,16,512]{3,2,1,0:T(8,128)}, u32[]{:S(2)}) copy-start(f32[3,2,16,512]{3,2,1,0:T(8,128)} %param.9) | copy-start | bytes 589828
  893.6 57.8 %copy-start.3 = (f32[3,2,16,512]{3,2,1,0:T(8,128)S(1)}, f32[3,2,16,512]{3,2,1,0:T(8,128)}, u32[]{:S(2)}) copy-start(f32[3,2,16,512]{3,2,1,0:T(8,128)} %multiply_subtract_fusion.5) | copy-start | bytes 589828
  893.6 57.8 %copy-start.4 = (f32[3,2,16,512]{3,2,1,0:T(8,128)S(1)}, f32[3,2,16,512]{3,2,1,0:T(8,128)}, u32[]{:S(2)}) copy-start(f32[3,2,16,512]{3,2,1,0:T(8,128)} %multiply_subtract_fusion.3) | copy-start | bytes 589828
  893.6 57.8 %copy-start.5 = (f32[3,2,16,512]{3,2,1,0:T(8,128)S(1)}, f32[3,2,16,512]{3,2,1,0:T(8,128)}, u32[]{:S(2)}) copy-start(f32[3,2,16,512]{3,2,1,0:T(8,128)} %multiply_add_fusion.2) | copy-start | bytes 589828
  893.6 57.8 %copy-start.7 = (f32[3,2,16,512]{3,2,1,0:T(8,128)S(1)}, f32[3,2,16,512]{3,2,1,0:T(8,128)}, u32[]{:S(2)}) copy-start(f32[3,2,16,512]{3,2,1,0:T(8,128)} %copy.106) | copy-start | bytes 589828
  893.6 57.8 %copy-start.8 = (f32[3,2,16,512]{3,2,1,0:T(8,128)S(1)}, f32[3,2,16,512]{3,2,1,0:T(8,128)}, u32[]{:S(2)}) copy-start(f32[3,2,16,512]{3,2,1,0:T(8,128)} %copy.112) | copy-start | bytes 589828
  (6 other events, 65.3 us)
